TPU v7x, 32 devices: a whole 2x2x4 slice. The times are simulated.
32 devices in a mesh: field: 4 (over x, core), slab: 8 (over z, y).
Axes of the slice: x: 2, y: 2, z: 4, core: 2. Of those that a mesh axis runs over, the one named last changes fastest.
Arguments:
- velocity_u: float32 [512, 512, 512], P('field', 'slab'), may hold values from -6 to 6
- velocity_v: float32 [512, 512, 512], P('field', 'slab'), may hold values from -6 to 6
- scalar_theta: float32 [512, 512, 512], P('field', 'slab'), may hold values from -6 to 6
Outputs:
- spectrum: float32 [4, 320, 320, 320], P('field', 'slab')
All inputs are finite; a program needn't handle non-finite values.
Results may differ from a plain program's by a relative error of at most 0.00029.
Values sent between devices are 32-bit elements; how exact they have to be, the bound alone decides.
A program may use at most 256 MiB of HBM per device.

v0:
```python
import jax
import jax.numpy as jnp
from jax import lax
from jax.sharding import PartitionSpec as P

N = 512
KEEP = 160


HIGH = lax.Precision.HIGHEST


def depth_table():
    places = jnp.arange(N, dtype=jnp.int32)
    waves = jnp.arange(KEEP, dtype=jnp.int32)
    phase = places[:, None] * waves[None, :] % N
    angle = phase.astype(jnp.float32) * (2.0 * jnp.pi / N)
    norm = 1.0 / jnp.sqrt(jnp.float32(N))
    return jnp.concatenate([jnp.cos(angle), -jnp.sin(angle)], axis=1) * norm


def plane_table():
    places = jnp.arange(N, dtype=jnp.int32)
    waves = jnp.arange(2 * KEEP, dtype=jnp.int32) - KEEP
    phase = waves[:, None] * places[None, :] % N
    angle = phase.astype(jnp.float32) * (2.0 * jnp.pi / N)
    norm = 1.0 / jnp.sqrt(jnp.float32(N))
    return jnp.concatenate([jnp.cos(angle), jnp.sin(angle)], axis=0) * norm


def combine(cos_part, sin_part):
    real_part = cos_part[..., :KEEP] + sin_part[..., KEEP:]
    imag_part = cos_part[..., KEEP:] - sin_part[..., :KEEP]
    return jnp.concatenate([real_part, imag_part], axis=-1)


def depth_form(values):
    return jnp.einsum("axyz,zc->axyc", values, depth_table(), precision=HIGH)


def first_form(piece):
    mixed = jnp.einsum("jx,axyc->ajyc", plane_table(), piece, precision=HIGH)
    return combine(mixed[:, : 2 * KEEP], mixed[:, 2 * KEEP :])


def second_form(piece):
    mixed = jnp.einsum("jy,akyc->akjc", plane_table(), piece, precision=HIGH)
    return combine(mixed[:, :, : 2 * KEEP], mixed[:, :, 2 * KEEP :])


def shards(velocity_u, velocity_v, scalar_theta):
    products = jnp.stack(
        [
            velocity_u * velocity_u,
            velocity_v * velocity_v,
            velocity_u * velocity_v,
            velocity_u * scalar_theta,
        ],
        axis=0,
    )
    partial_spec = depth_form(products)
    planes = first_form(
        lax.all_to_all(partial_spec, "field", split_axis=0, concat_axis=1, tiled=True)
    )
    result = second_form(lax.all_to_all(planes, "slab", split_axis=1, concat_axis=2, tiled=True))
    local_rows = result.shape[1]
    first_index = lax.axis_index("slab") * local_rows + jnp.arange(local_rows, dtype=jnp.int32)
    second_index = jnp.arange(2 * KEEP, dtype=jnp.int32)
    column_index = jnp.arange(2 * KEEP, dtype=jnp.int32)
    zero_mode = (
        (first_index[:, None, None] == KEEP)
        & (second_index[None, :, None] == KEEP)
        & (column_index[None, None, :] == 0)
    )
    return jnp.where(zero_mode[None], jnp.float32(0.0), result)


def solution(mesh):
    in_specs = (P("field", "slab", None), P("field", "slab", None), P("field", "slab", None))
    out_specs = P("field", "slab", None, None)
    return jax.shard_map(shards, mesh=mesh, in_specs=in_specs, out_specs=out_specs, check_vma=False)
```

profile of v0, /device:TPU:0, one launch (start us, length us, event | category | flops | bytes accessed | tf_op | source)
XLA Modules:
  0.0 1709.1 jit_solution(4037053764958189074)
XLA Ops:
  0.0 1.3 sine_negate_fusion
  1.3 0.1 fusion.66
  1.4 46.9 %multiply_bitcast_fusion.2 = (f32[1,128,64,512]{3,1,2,0:T(8,128)}, f32[1,128,64,512]{3,1,2,0:T(8,128)}, f32[1,128,64,512]{3,1,2,0:T(8,128)}, f32[1,128,64,512]{3,1,2,0:T(8,128)}) fusion(f32[128,64,512]{2,1,0:T(8,128)} %param.3, f32[128,64,512]{2,1,0:T(8,128)} %param.4, f32[128,64,512]{2,1,0:T(8,128)} %param.5), kind=kLoop, calls=%fused_computation.18 | loop fusion | flops 16777216 | bytes 117440512 | tf_op jit(solution)/shard_map/stack | solution.py:52
  48.3 76.5 %fusion = f32[4,128,64,320]{1,3,2,0:T(8,128)} fusion(f32[1,128,64,512]{3,1,2,0:T(8,128)} %get-tuple-element.12, f32[1,128,64,512]{3,1,2,0:T(8,128)} %get-tuple-element.10, f32[1,128,64,512]{3,1,2,0:T(8,128)} %get-tuple-element.11, f32[1,128,64,512]{3,1,2,0:T(8,128)} %get-tuple-element.9, f32[512,320,1,1]{0,1,3,2:T(8,128)S(1)} %fusion.66), kind=kOutput, calls=%fused_computation | convolution fusion | flops 64474841088 | bytes 109707264 | tf_op jit(solution)/shard_map/axyz,zc->axyc/dot_general | solution.py:38
  124.8 11.4 all-to-all-start
  136.3 2.6 fusion.34
  138.9 0.1 fusion.68
  139.1 450.7 %all-to-all-done = f32[4,128,64,320]{1,3,2,0:T(8,128)} async-done(((f32[4,128,64,320]{1,3,2,0:T(8,128)}), f32[4,128,64,320]{1,3,2,0:T(8,128)}, u32[]{:S(2)}, u32[]{:S(2)}) %all-to-all-start) | async-done | bytes 41943072 | tf_op jit(solution)/shard_map/all_to_all | solution.py:63
  589.7 107.1 %fusion.11 = f32[1,640,64,320]{1,3,2,0:T(8,128)} fusion(f32[4,128,64,320]{1,3,2,0:T(8,128)} %all-to-all-done, f32[640,512,1]{1,0,2:T(8,128)S(1)} %fusion.68), kind=kOutput, calls=%fused_computation.12 | convolution fusion | flops 80530636800 | bytes 95682560 | tf_op jit(solution)/shard_map/jx,axyc->ajyc/dot_general | solution.py:42
  696.8 33.2 %slice_add_fusion = (f32[1,320,64,160]{1,3,2,0:T(8,128)}, f32[1,320,64,160]{1,3,2,0:T(8,128)}) fusion(f32[1,640,64,320]{1,3,2,0:T(8,128)} %fusion.11), kind=kLoop, calls=%fused_computation.20 | loop fusion | flops 6553600 | bytes 78643200 | tf_op jit(solution)/shard_map/add | solution.py:32
  730.0 21.9 %pad_maximum_fusion = f32[1,320,64,320]{1,3,2,0:T(8,128)} fusion(f32[1,320,64,160]{1,3,2,0:T(8,128)} %get-tuple-element.6, f32[1,320,64,160]{1,3,2,0:T(8,128)} %get-tuple-element.5), kind=kLoop, calls=%fused_computation.11 | loop fusion | flops 6553600 | bytes 52428800 | tf_op jit(solution)/shard_map/concatenate | solution.py:34
  751.8 33.2 %copy.36 = f32[1,320,64,320]{3,2,0,1:T(8,128)} copy(f32[1,320,64,320]{1,3,2,0:T(8,128)} %pad_maximum_fusion) | data formatting | bytes 52428800 | tf_op jit(solution)/shard_map/concatenate | solution.py:34
  785.0 6.9 all-to-all-start.1
  792.0 0.1 fusion.70
  792.1 0.1 broadcast_and_fusion
  792.2 678.6 %all-to-all-done.1 = f32[1,320,64,320]{3,2,0,1:T(8,128)} async-done(((f32[1,320,64,320]{3,2,0,1:T(8,128)}), f32[1,320,64,320]{3,2,0,1:T(8,128)}, u32[]{:S(2)}, u32[]{:S(2)}) %all-to-all-start.1) | async-done | bytes 26214432 | tf_op jit(solution)/shard_map/all_to_all | solution.py:65
  1470.8 22.2 %copy.37 = f32[1,40,8,64,320]{4,3,2,1,0:T(8,128)} copy(f32[1,40,8,64,320]{4,3,1,2,0:T(8,128)} %bitcast.11) | data formatting | bytes 52428800 | tf_op jit(solution)/shard_map/all_to_all | solution.py:65
  1493.0 173.3 %convolution_bitcast_fusion = f32[1,40,640,320]{2,3,1,0:T(8,128)} fusion(f32[40,512,320]{2,1,0:T(8,128)} %bitcast.63, f32[640,512,1]{1,0,2:T(8,128)S(1)} %fusion.70), kind=kOutput, calls=%fused_computation.21 | convolution fusion | flops 50331648000 | bytes 60293120 | tf_op jit(solution)/shard_map/jy,akyc->akjc/dot_general | solution.py:47
  1666.3 14.1 slice_add_fusion.1
  1680.4 7.3 maximum_select_fusion
  1687.7 21.0 %copy.39 = f32[1,40,320,320]{3,2,1,0:T(8,128)} copy(f32[1,40,320,320]{2,3,1,0:T(8,128)} %maximum_select_fusion) | data formatting | bytes 32768000 | tf_op jit(solution)/shard_map/jit(_where)/select_n | solution.py:75
  (4 shorter events, 0.0 us)
Async XLA Ops:
  124.8 464.9 %all-to-all-start = ((f32[4,128,64,320]{1,3,2,0:T(8,128)}), f32[4,128,64,320]{1,3,2,0:T(8,128)}, u32[]{:S(2)}, u32[]{:S(2)}) async-start(f32[4,128,64,320]{1,3,2,0:T(8,128)} %fusion), calls=%async_computation | async-start | bytes 83886080 | tf_op jit(solution)/shard_map/all_to_all | solution.py:63
  785.0 685.8 %all-to-all-start.1 = ((f32[1,320,64,320]{3,2,0,1:T(8,128)}), f32[1,320,64,320]{3,2,0,1:T(8,128)}, u32[]{:S(2)}, u32[]{:S(2)}) async-start(f32[1,320,64,320]{3,2,0,1:T(8,128)} %copy.36), calls=%async_computation.1 | async-start | bytes 62914560 | tf_op jit(solution)/shard_map/all_to_all | solution.py:65
where the time goes:
time: 1720 us; the launch traced here: 1710 us
  waiting for transfers between devices  1130 us (66%)
  matrix products  357 us (21%)
  other arithmetic  128 us (7%)
  local copies, waits for them, and re-layouts  76.4 us (4%)
  starting transfers between devices  18.3 us (1%)
    all_to_all x1, waiting for transfers between devices, shards(): lax.all_to_all(planes, 'slab', split_axis=1, concat_axis=2, tiled=True)  679 us
    all_to_all x1, waiting for transfers between devices, shards(): lax.all_to_all(partial_spec, 'field', split_axis=0, concat_axis=1, tiled=...  451 us
    dot_general x1, matrix products, second_form(): mixed = jnp.einsum('jy,akyc->akjc', plane_table(), piece, precision=HIGH)  173 us
    dot_general x1, matrix products, first_form(): mixed = jnp.einsum('jx,axyc->ajyc', plane_table(), piece, precision=HIGH)  107 us
    dot_general x1, matrix products, depth_form(): return jnp.einsum('axyz,zc->axyc', values, depth_table(), precision=HIGH)  76.5 us
    add x2, other arithmetic, combine(): real_part = cos_part[..., :KEEP] + sin_part[..., KEEP:]  47.2 us
    another operation x1, other arithmetic, shards(): jnp.stack([velocity_u * velocity_u, velocity_v * velocity_v, velocity_u *...  46.9 us
  transfers between devices with their start and end apart: 2, of which 2 were waited for; matrix products, arithmetic and copies ran while one was open for 0% of the time, Pallas kernels for 0%

commit v1 on v0

v1 whole, which is shorter than its diff:
```python
import jax
import jax.numpy as jnp
from jax import lax
from jax.experimental import pallas as pl
from jax.experimental.pallas import tpu as pltpu
from jax.sharding import PartitionSpec as P

N = 512
KEEP = 160
CHUNKS = 8
KBLOCK = 4
HIGH = lax.Precision.HIGH


def waves_of(phase):
    angle = (phase % N).astype(jnp.float32) * (2.0 * jnp.pi / N)
    norm = 1.0 / jnp.sqrt(jnp.float32(N))
    return jnp.cos(angle) * norm, jnp.sin(angle) * norm


def depth_table():
    places = jnp.arange(N, dtype=jnp.int32)
    waves = jnp.arange(KEEP, dtype=jnp.int32)
    c, s = waves_of(places[:, None] * waves[None, :])
    return jnp.stack([c, -s], axis=0)


def complex_table(phase):
    c, s = waves_of(phase)
    return jnp.stack([jnp.stack([c, s]), jnp.stack([-s, c])])


def halves(x):
    high = x.astype(jnp.bfloat16)
    return high, (x - high.astype(jnp.float32)).astype(jnp.bfloat16)


def second_kernel(table_ref, piece_ref, *rest):
    out_ref = rest[-1]
    tables = [halves(table_ref[r]) for r in range(2)]
    for k in range(piece_ref.shape[0]):
        high, low = halves(piece_ref[k])
        for r in range(2):
            t_high, t_low = tables[r]
            value = jnp.dot(t_high, high, preferred_element_type=jnp.float32)
            value += jnp.dot(t_high, low, preferred_element_type=jnp.float32)
            value += jnp.dot(t_low, high, preferred_element_type=jnp.float32)
            cols = slice(r * KEEP, (r + 1) * KEEP)
            if len(rest) > 1:
                value += rest[0][k, :, cols]
            out_ref[k, :, cols] = value


def second(table, piece, total):
    rows, depth, _ = piece.shape
    wide = 2 * KEEP
    block = pl.BlockSpec((KBLOCK, wide, wide), lambda g: (g, 0, 0))
    specs = [
        pl.BlockSpec((2, wide, depth), lambda g: (0, 0, 0)),
        pl.BlockSpec((KBLOCK, depth, KEEP), lambda g: (g, 0, 0)),
    ]
    args = [table, piece]
    if total is not None:
        specs.append(block)
        args.append(total)
    return pl.pallas_call(
        second_kernel,
        out_shape=jax.ShapeDtypeStruct((rows, wide, wide), jnp.float32),
        grid=(rows // KBLOCK,),
        in_specs=specs,
        out_specs=block,
        input_output_aliases={2: 0} if total is not None else {},
        cost_estimate=pl.CostEstimate(
            flops=12 * rows * wide * depth * KEEP,
            bytes_accessed=4 * rows * (2 * wide * wide + depth * 256),
            transcendentals=0,
        ),
        compiler_params=pltpu.CompilerParams(vmem_limit_bytes=24 * 2**20),
    )(*args)


def make_shards(fields, slabs):
    def shards(u, v, t):
        f = lax.axis_index("field")
        xs, ys, _ = u.shape
        rows = 2 * KEEP // slabs
        step = ys // CHUNKS
        size = step * KEEP
        zt = depth_table()
        k = jnp.arange(2 * KEEP, dtype=jnp.int32) - KEEP
        rounds = jnp.arange(fields, dtype=jnp.int32)
        xg = ((f ^ rounds) * xs)[:, None] + jnp.arange(xs, dtype=jnp.int32)[None]
        xt = complex_table(k[:, None, None] * xg[None])
        xt = xt.reshape(2, 2, slabs, rows, fields, xs)
        yg = jnp.arange(N, dtype=jnp.int32)
        yt = complex_table(k[:, None] * yg[None]).reshape(2, 2, 2 * KEEP, slabs, CHUNKS, step)
        parts = []
        for i in range(CHUNKS):
            uc, vc, tc = (lax.slice_in_dim(a, i * step, (i + 1) * step, axis=1) for a in (u, v, t))
            got = []
            for m in range(fields):
                q = f ^ m
                left = jnp.where(q == 1, vc, uc)
                right = jnp.where(q == 0, uc, jnp.where(q == 3, tc, vc))
                part = jnp.einsum("xyz,rzc->rycx", left * right, zt, precision=HIGH)
                if m:
                    part = lax.ppermute(part, "field", [(a, a ^ m) for a in range(fields)])
                got.append(part)
            parts.append(got)
        total = None
        for i in range(CHUNKS):
            have = jnp.stack(parts[i], axis=0)
            mixed = jnp.einsum("RrSKmx,mrycx->SRKyc", xt, have, precision=HIGH)
            mixed = mixed.reshape(slabs, 2, rows, size)
            mixed = lax.all_to_all(mixed, "slab", split_axis=0, concat_axis=0, tiled=True)
            mixed = mixed.reshape(slabs, 2, rows, step, KEEP).transpose(2, 0, 1, 3, 4)
            mixed = mixed.reshape(rows, slabs * 2 * step, KEEP)
            table = yt[:, :, :, :, i].transpose(0, 2, 3, 1, 4).reshape(2, 2 * KEEP, -1)
            total = second(table, mixed, total)
        row = KEEP - lax.axis_index("slab") * rows
        mine = (row >= 0) & (row < rows)
        at = (0, jnp.clip(row, 0, rows - 1), KEEP, 0)
        total = total[None]
        old = lax.dynamic_slice(total, at, (1, 1, 1, 1))
        return lax.dynamic_update_slice(total, jnp.where(mine, jnp.float32(0.0), old), at)

    return shards


def solution(mesh):
    spec = P("field", "slab", None)
    fields = mesh.shape["field"]
    return jax.shard_map(
        make_shards(fields, mesh.shape["slab"]),
        mesh=mesh,
        in_specs=(spec, spec, spec),
        out_specs=P("field", "slab", None, None),
        check_vma=False,
    )
```

time: 1720 us -> 1010 us (0.59)
  waiting for transfers between devices: 1130 us -> 339 us
  matrix products: 357 us -> 152 us
  Pallas kernels: 0 us -> 155 us
  local copies, waits for them, and re-layouts: 76.4 us -> 190 us
  starting transfers between devices: 18.3 us -> 66.3 us
  other arithmetic: 128 us -> 93.7 us
    all_to_all x2 -> x8, waiting for transfers between devices: 1130 us -> 0.02 us  [shards(): lax.all_to_all(mixed, 'slab', split_axis=0, concat_axis=0, tiled=True)]
    ppermute x0 -> x24, waiting for transfers between devices: none -> 339 us  [shards(): part = lax.ppermute(part, 'field', [(a, a ^ m) for a in range(fields)])]
    dot_general x3 -> x40, matrix products: 357 us -> 152 us  [the longest x32 80.8 us: shards(): part = jnp.einsum('xyz,rzc->rycx', left * right, zt, precision=HIGH)]
    pallas_call x0 -> x8, Pallas kernels: none -> 155 us  [second(): pl.pallas_call(second_kernel, out_shape=jax.ShapeDtypeStruct((rows, wide,...]
    reshape x0 -> x32, local copies, waits for them, and re-layouts: none -> 143 us  [the longest x16 91.7 us: shards(): mixed = mixed.reshape(slabs, 2, rows, step, KEEP).transpose(2, 0, 1, 3, 4)]
    mul x0 -> x13, other arithmetic: none -> 92.1 us  [the longest x9 86.2 us: shards(): part = jnp.einsum('xyz,rzc->rycx', left * right, zt, precision=HIGH)]
    add x2 -> x1, other arithmetic: 47.2 us -> 0.07 us  [shards(): xg = ((f ^ rounds) * xs)[:, None] + jnp.arange(xs, dtype=jnp.int32)[None]]
    another operation x1, other arithmetic: 46.9 us -> 0.24 us  [complex_table(): return jnp.stack([jnp.stack([c, s]), jnp.stack([-s, c])])]
  transfers between devices with their start and end apart: 2 -> 32, of which waited for: 2 -> 15; matrix products, arithmetic and copies ran while one was open for 0% -> 39% of each run, Pallas kernels for 0% -> 0%
where the time goes in v1:
time: 1010 us; the launch traced here: 998 us
  waiting for transfers between devices  339 us (34%)
  local copies, waits for them, and re-layouts  190 us (19%)
  Pallas kernels  155 us (15%)
  matrix products  152 us (15%)
  other arithmetic  93.7 us (9%)
  starting transfers between devices  66.3 us (7%)
    ppermute x24, waiting for transfers between devices, shards(): part = lax.ppermute(part, 'field', [(a, a ^ m) for a in range(fields)])  339 us
    pallas_call x8, Pallas kernels, second(): pl.pallas_call(second_kernel, out_shape=jax.ShapeDtypeStruct((rows, wide,...  155 us
    reshape x16, local copies, waits for them, and re-layouts, shards(): mixed = mixed.reshape(slabs, 2, rows, step, KEEP).transpose(2, 0, 1, 3, 4)  91.7 us
    mul x9, other arithmetic, shards(): part = jnp.einsum('xyz,rzc->rycx', left * right, zt, precision=HIGH)  86.2 us
    dot_general x32, matrix products, shards(): part = jnp.einsum('xyz,rzc->rycx', left * right, zt, precision=HIGH)  80.8 us
    dot_general x8, matrix products, shards(): mixed = jnp.einsum('RrSKmx,mrycx->SRKyc', xt, have, precision=HIGH)  71.1 us
    all_to_all x8, starting transfers between devices, shards(): lax.all_to_all(mixed, 'slab', split_axis=0, concat_axis=0, tiled=True)  48.7 us
    reshape x8, local copies, waits for them, and re-layouts, shards(): mixed = mixed.reshape(slabs, 2, rows, size)  46.7 us
  transfers between devices with their start and end apart: 32, of which 15 were waited for; matrix products, arithmetic and copies ran while one was open for 39% of the time, Pallas kernels for 0%

profile of v1, /device:TPU:0, one launch (start us, length us, event | category | flops | bytes accessed | tf_op | source)
XLA Modules:
  0.0 997.5 jit_solution(3064039782989703099)
XLA Ops:
  1.3 9.9 select_multiply_fusion.2
  17.0 7.6 select_multiply_fusion.3
  30.2 12.5 %select_multiply_fusion.19 = (f32[128,8,512]{2,1,0:T(8,128)}, f32[128,8,512]{2,1,0:T(8,128)}, f32[128,8,512]{2,1,0:T(8,128)}, f32[128,8,512]{2,1,0:T(8,128)S(1)}) fusion(f32[128,64,512]{2,1,0:T(8,128)} %param.5, f32[128,64,512]{2,1,0:T(8,128)} %param.3, f32[128,64,512]{2,1,0:T(8,128)} %param.4, pred[]{:T(512)S(6)} %eq.32, pred[]{:T(512)S(6)} %eq.31, pred[]{:T(512)S(6)} %eq.30), kind=kLoop, calls=%fused_computation.149 | loop fusion | flops 8388608 | bytes 33554436 | tf_op jit(solution)/shard_map/mul | solution.py:105
  47.8 26.8 %collective-permute-done.1 = f32[2,8,160,128]{3,2,1,0:T(8,128)S(1)} collective-permute-done((f32[2,8,160,128]{3,2,1,0:T(8,128)S(1)}, f32[2,8,160,128]{3,2,1,0:T(8,128)S(1)}, u32[]{:S(2)}, u32[]{:S(2)}) %collective-permute-start.1) | collective-permute-done | bytes 1310752 | tf_op jit(solution)/shard_map/ppermute | solution.py:107
  74.6 10.2 %fusion.16 = f32[8,2,40,8,160]{4,2,0,1,3:T(8,128)S(1)} fusion(f32[1,1,8,40,4,128]{5,3,1,4,2,0:T(8,128)S(1)} %get-tuple-element.50, f32[1,1,8,40,4,128]{5,3,1,4,2,0:T(8,128)S(1)} %get-tuple-element.49, f32[1,1,8,40,4,128]{5,3,1,4,2,0:T(8,128)S(1)} %get-tuple-element.48, f32[1,2,8,160,128]{4,3,2,1,0:T(8,128)} %bitcast.17, ...), kind=kOutput, calls=%fused_computation.26 | convolution fusion | flops 5039063040 | bytes 10485760 | tf_op jit(solution)/shard_map/RrSKmx,mrycx->SRKyc/dot_general | solution.py:113
  96.1 6.7 all-to-all-start
  107.6 10.7 %select_multiply_fusion.1 = (f32[128,8,512]{2,1,0:T(8,128)}, f32[128,8,512]{2,1,0:T(8,128)S(1)}, f32[128,8,512]{2,1,0:T(8,128)}, f32[128,8,512]{2,1,0:T(8,128)}) fusion(f32[128,64,512]{2,1,0:T(8,128)} %param.5, f32[128,64,512]{2,1,0:T(8,128)} %param.3, f32[128,64,512]{2,1,0:T(8,128)} %param.4, pred[]{:T(512)S(6)} %eq.38, pred[]{:T(512)S(6)} %eq.37, ...), kind=kLoop, calls=%fused_computation.131 | loop fusion | flops 8388608 | bytes 27262982 | tf_op jit(solution)/shard_map/mul | solution.py:105
  126.4 11.3 %collective-permute-done.5 = f32[2,8,160,128]{3,2,1,0:T(8,128)S(1)} collective-permute-done((f32[2,8,160,128]{3,2,1,0:T(8,128)S(1)}, f32[2,8,160,128]{3,2,1,0:T(8,128)S(1)}, u32[]{:S(2)}, u32[]{:S(2)}) %collective-permute-start.5) | collective-permute-done | bytes 1310752 | tf_op jit(solution)/shard_map/ppermute | solution.py:107
  137.7 28.1 %collective-permute-done.4 = f32[2,8,160,128]{3,2,1,0:T(8,128)S(1)} collective-permute-done((f32[2,8,160,128]{3,2,1,0:T(8,128)S(1)}, f32[2,8,160,128]{3,2,1,0:T(8,128)S(1)}, u32[]{:S(2)}, u32[]{:S(2)}) %collective-permute-start.4) | collective-permute-done | bytes 1310752 | tf_op jit(solution)/shard_map/ppermute | solution.py:107
  165.9 8.7 fusion.19
  191.8 10.1 %select_multiply_fusion = (f32[128,8,512]{2,1,0:T(8,128)}, f32[128,8,512]{2,1,0:T(8,128)S(1)}, f32[128,8,512]{2,1,0:T(8,128)}, f32[128,8,512]{2,1,0:T(8,128)S(1)}) fusion(f32[128,64,512]{2,1,0:T(8,128)} %param.5, f32[128,64,512]{2,1,0:T(8,128)} %param.3, f32[128,64,512]{2,1,0:T(8,128)} %param.4, pred[]{:T(512)S(6)} %eq.41, pred[]{:T(512)S(6)} %eq.40, ...), kind=kLoop, calls=%fused_computation.130 | loop fusion | flops 8388608 | bytes 27262982 | tf_op jit(solution)/shard_map/mul | solution.py:105
  213.5 21.9 %collective-permute-done.8 = f32[2,8,160,128]{3,2,1,0:T(8,128)S(1)} collective-permute-done((f32[2,8,160,128]{3,2,1,0:T(8,128)S(1)}, f32[2,8,160,128]{3,2,1,0:T(8,128)S(1)}, u32[]{:S(2)}, u32[]{:S(2)}) %collective-permute-start.8) | collective-permute-done | bytes 1310752 | tf_op jit(solution)/shard_map/ppermute | solution.py:107
  235.4 28.2 %collective-permute-done.7 = f32[2,8,160,128]{3,2,1,0:T(8,128)S(1)} collective-permute-done((f32[2,8,160,128]{3,2,1,0:T(8,128)S(1)}, f32[2,8,160,128]{3,2,1,0:T(8,128)S(1)}, u32[]{:S(2)}, u32[]{:S(2)}) %collective-permute-start.7) | collective-permute-done | bytes 1310752 | tf_op jit(solution)/shard_map/ppermute | solution.py:107
  263.6 8.7 fusion.22
  292.2 9.2 select_multiply_fusion.7
  309.8 12.5 %collective-permute-done.11 = f32[2,8,160,128]{3,2,1,0:T(8,128)S(1)} collective-permute-done((f32[2,8,160,128]{3,2,1,0:T(8,128)S(1)}, f32[2,8,160,128]{3,2,1,0:T(8,128)S(1)}, u32[]{:S(2)}, u32[]{:S(2)}) %collective-permute-start.11) | collective-permute-done | bytes 1310752 | tf_op jit(solution)/shard_map/ppermute | solution.py:107
  322.4 28.3 %collective-permute-done.10 = f32[2,8,160,128]{3,2,1,0:T(8,128)S(1)} collective-permute-done((f32[2,8,160,128]{3,2,1,0:T(8,128)S(1)}, f32[2,8,160,128]{3,2,1,0:T(8,128)S(1)}, u32[]{:S(2)}, u32[]{:S(2)}) %collective-permute-start.10) | collective-permute-done | bytes 1310752 | tf_op jit(solution)/shard_map/ppermute | solution.py:107
  350.7 8.9 fusion.25
  370.8 6.2 all-to-all-start.3
  377.0 7.7 select_multiply_fusion.6
  393.8 10.9 %select_multiply_fusion.4 = (f32[128,8,512]{2,1,0:T(8,128)}, f32[128,8,512]{2,1,0:T(8,128)}, f32[128,8,512]{2,1,0:T(8,128)}, f32[128,8,512]{2,1,0:T(8,128)S(1)}) fusion(f32[128,64,512]{2,1,0:T(8,128)} %param.5, f32[128,64,512]{2,1,0:T(8,128)} %param.3, f32[128,64,512]{2,1,0:T(8,128)} %param.4, pred[]{:T(512)S(6)} %eq.41, pred[]{:T(512)S(6)} %eq.40, ...), kind=kLoop, calls=%fused_computation.134 | loop fusion | flops 8388608 | bytes 27262982 | tf_op jit(solution)/shard_map/mul | solution.py:105
  407.1 11.0 %collective-permute-done.14 = f32[2,8,160,128]{3,2,1,0:T(8,128)S(1)} collective-permute-done((f32[2,8,160,128]{3,2,1,0:T(8,128)S(1)}, f32[2,8,160,128]{3,2,1,0:T(8,128)S(1)}, u32[]{:S(2)}, u32[]{:S(2)}) %collective-permute-start.14) | collective-permute-done | bytes 1310752 | tf_op jit(solution)/shard_map/ppermute | solution.py:107
  418.0 28.2 %collective-permute-done.13 = f32[2,8,160,128]{3,2,1,0:T(8,128)S(1)} collective-permute-done((f32[2,8,160,128]{3,2,1,0:T(8,128)S(1)}, f32[2,8,160,128]{3,2,1,0:T(8,128)S(1)}, u32[]{:S(2)}, u32[]{:S(2)}) %collective-permute-start.13) | collective-permute-done | bytes 1310752 | tf_op jit(solution)/shard_map/ppermute | solution.py:107
  446.3 8.5 fusion.28
  476.3 7.6 select_multiply_fusion.5
  492.6 14.1 %collective-permute-done.17 = f32[2,8,160,128]{3,2,1,0:T(8,128)S(1)} collective-permute-done((f32[2,8,160,128]{3,2,1,0:T(8,128)S(1)}, f32[2,8,160,128]{3,2,1,0:T(8,128)S(1)}, u32[]{:S(2)}, u32[]{:S(2)}) %collective-permute-start.17) | collective-permute-done | bytes 1310752 | tf_op jit(solution)/shard_map/ppermute | solution.py:107
  506.7 28.4 %collective-permute-done.16 = f32[2,8,160,128]{3,2,1,0:T(8,128)S(1)} collective-permute-done((f32[2,8,160,128]{3,2,1,0:T(8,128)S(1)}, f32[2,8,160,128]{3,2,1,0:T(8,128)S(1)}, u32[]{:S(2)}, u32[]{:S(2)}) %collective-permute-start.16) | collective-permute-done | bytes 1310752 | tf_op jit(solution)/shard_map/ppermute | solution.py:107
  535.0 8.9 fusion.31
  555.1 6.1 all-to-all-start.5
  574.4 21.9 %collective-permute-done.20 = f32[2,8,160,128]{3,2,1,0:T(8,128)S(1)} collective-permute-done((f32[2,8,160,128]{3,2,1,0:T(8,128)S(1)}, f32[2,8,160,128]{3,2,1,0:T(8,128)S(1)}, u32[]{:S(2)}, u32[]{:S(2)}) %collective-permute-start.20) | collective-permute-done | bytes 1310752 | tf_op jit(solution)/shard_map/ppermute | solution.py:107
  596.3 28.2 %collective-permute-done.19 = f32[2,8,160,128]{3,2,1,0:T(8,128)S(1)} collective-permute-done((f32[2,8,160,128]{3,2,1,0:T(8,128)S(1)}, f32[2,8,160,128]{3,2,1,0:T(8,128)S(1)}, u32[]{:S(2)}, u32[]{:S(2)}) %collective-permute-start.19) | collective-permute-done | bytes 1310752 | tf_op jit(solution)/shard_map/ppermute | solution.py:107
  624.5 8.7 fusion.34
  644.5 6.2 all-to-all-start.6
  662.2 21.8 %collective-permute-done.23 = f32[2,8,160,128]{3,2,1,0:T(8,128)S(1)} collective-permute-done((f32[2,8,160,128]{3,2,1,0:T(8,128)S(1)}, f32[2,8,160,128]{3,2,1,0:T(8,128)S(1)}, u32[]{:S(2)}, u32[]{:S(2)}) %collective-permute-start.23) | collective-permute-done | bytes 1310752 | tf_op jit(solution)/shard_map/ppermute | solution.py:107
  683.9 28.3 %collective-permute-done.22 = f32[2,8,160,128]{3,2,1,0:T(8,128)S(1)} collective-permute-done((f32[2,8,160,128]{3,2,1,0:T(8,128)S(1)}, f32[2,8,160,128]{3,2,1,0:T(8,128)S(1)}, u32[]{:S(2)}, u32[]{:S(2)}) %collective-permute-start.22) | collective-permute-done | bytes 1310752 | tf_op jit(solution)/shard_map/ppermute | solution.py:107
  712.3 8.6 fusion.37
  732.2 6.2 all-to-all-start.7
  747.4 6.1 reshape.402
  817.6 6.3 reshape.426
  829.6 6.1 reshape.430
  839.1 13.8 %shard_map.37.rest_0_ = f32[40,320,320]{2,1,0:T(8,128)} custom-call(f32[2,320,128]{2,1,0:T(8,128)S(1)} %copy.107.table_ref, f32[40,128,160]{2,1,0:T(8,128)S(1)} %bitcast.489), custom_call_target="tpu_custom_call" | custom-call | flops 3145728000 | bytes 38010880 | tf_op jit(solution)/shard_map/pallas_call | solution.py:66
  853.0 20.2 %shard_map.38.rest_0_ = f32[40,320,320]{2,1,0:T(8,128)} custom-call(f32[2,320,128]{2,1,0:T(8,128)S(1)} %copy.108.table_ref, f32[40,128,160]{2,1,0:T(8,128)S(1)} %bitcast.510, f32[40,320,320]{2,1,0:T(8,128)} %shard_map.37.rest_0_), custom_call_target="tpu_custom_call", output_to_operand_aliasing={{}: (2, {})} | custom-call | flops 3145728000 | bytes 38010880 | tf_op jit(solution)/shard_map/pallas_call | solution.py:66
  873.2 20.2 %shard_map.39.rest_0_ = f32[40,320,320]{2,1,0:T(8,128)} custom-call(f32[2,320,128]{2,1,0:T(8,128)S(1)} %copy.109.table_ref, f32[40,128,160]{2,1,0:T(8,128)S(1)} %bitcast.507, f32[40,320,320]{2,1,0:T(8,128)} %shard_map.38.rest_0_), custom_call_target="tpu_custom_call", output_to_operand_aliasing={{}: (2, {})} | custom-call | flops 3145728000 | bytes 38010880 | tf_op jit(solution)/shard_map/pallas_call | solution.py:66
  893.3 20.2 %shard_map.40.rest_0_ = f32[40,320,320]{2,1,0:T(8,128)} custom-call(f32[2,320,128]{2,1,0:T(8,128)S(1)} %copy.110.table_ref, f32[40,128,160]{2,1,0:T(8,128)S(1)} %bitcast.504, f32[40,320,320]{2,1,0:T(8,128)} %shard_map.39.rest_0_), custom_call_target="tpu_custom_call", output_to_operand_aliasing={{}: (2, {})} | custom-call | flops 3145728000 | bytes 38010880 | tf_op jit(solution)/shard_map/pallas_call | solution.py:66
  913.5 20.2 %shard_map.41.rest_0_ = f32[40,320,320]{2,1,0:T(8,128)} custom-call(f32[2,320,128]{2,1,0:T(8,128)S(1)} %copy.111.table_ref, f32[40,128,160]{2,1,0:T(8,128)S(1)} %bitcast.501, f32[40,320,320]{2,1,0:T(8,128)} %shard_map.40.rest_0_), custom_call_target="tpu_custom_call", output_to_operand_aliasing={{}: (2, {})} | custom-call | flops 3145728000 | bytes 38010880 | tf_op jit(solution)/shard_map/pallas_call | solution.py:66
  933.7 20.2 %shard_map.42.rest_0_ = f32[40,320,320]{2,1,0:T(8,128)} custom-call(f32[2,320,128]{2,1,0:T(8,128)S(1)} %copy.112.table_ref, f32[40,128,160]{2,1,0:T(8,128)S(1)} %bitcast.498, f32[40,320,320]{2,1,0:T(8,128)} %shard_map.41.rest_0_), custom_call_target="tpu_custom_call", output_to_operand_aliasing={{}: (2, {})} | custom-call | flops 3145728000 | bytes 38010880 | tf_op jit(solution)/shard_map/pallas_call | solution.py:66
  953.9 20.1 %shard_map.43.rest_0_ = f32[40,320,320]{2,1,0:T(8,128)} custom-call(f32[2,320,128]{2,1,0:T(8,128)S(1)} %copy.113.table_ref, f32[40,128,160]{2,1,0:T(8,128)S(1)} %bitcast.495, f32[40,320,320]{2,1,0:T(8,128)} %shard_map.42.rest_0_), custom_call_target="tpu_custom_call", output_to_operand_aliasing={{}: (2, {})} | custom-call | flops 3145728000 | bytes 38010880 | tf_op jit(solution)/shard_map/pallas_call | solution.py:66
  974.0 20.0 %shard_map.44 = f32[40,320,320]{2,1,0:T(8,128)} custom-call(f32[2,320,128]{2,1,0:T(8,128)S(1)} %copy.114.table_ref, f32[40,128,160]{2,1,0:T(8,128)S(1)} %bitcast.492, f32[40,320,320]{2,1,0:T(8,128)} %shard_map.43.rest_0_), custom_call_target="tpu_custom_call", output_to_operand_aliasing={{}: (2, {})} | custom-call | flops 3145728000 | bytes 38010880 | tf_op jit(solution)/shard_map/pallas_call | solution.py:66
  (220 shorter events, 294.7 us)
Async XLA Ops:
  14.6 33.2 %collective-permute-start.2 = (f32[2,8,160,128]{3,2,1,0:T(8,128)}, f32[2,8,160,128]{3,2,1,0:T(8,128)}, u32[]{:S(2)}, u32[]{:S(2)}) collective-permute-start(f32[2,8,160,128]{3,2,1,0:T(8,128)} %fusion.145), channel_id=1, source_target_pairs={{0,24},{8,16},{16,8},{24,0},{1,25},{9,17},{17,9},{25,1},{2,26},{10... | collective-permute-start | bytes 3932168 | tf_op jit(solution)/shard_map/ppermute | solution.py:107
  27.0 47.7 %collective-permute-start.1 = (f32[2,8,160,128]{3,2,1,0:T(8,128)S(1)}, f32[2,8,160,128]{3,2,1,0:T(8,128)S(1)}, u32[]{:S(2)}, u32[]{:S(2)}) collective-permute-start(f32[2,8,160,128]{3,2,1,0:T(8,128)S(1)} %fusion.142), channel_id=1, source_target_pairs={{0,16},{8,24},{16,0},{24,8},{1,17},{9,25},{17,1},{25,9},{2,18},{10... | collective-permute-start | bytes 3932168 | tf_op jit(solution)/shard_map/ppermute | solution.py:107
  30.0 44.7 %collective-permute-start = (f32[2,8,160,128]{3,2,1,0:T(8,128)S(1)}, f32[2,8,160,128]{3,2,1,0:T(8,128)S(1)}, u32[]{:S(2)}, u32[]{:S(2)}) collective-permute-start(f32[2,8,160,128]{3,2,1,0:T(8,128)S(1)} %fusion.139), channel_id=1, source_target_pairs={{0,8},{8,0},{16,24},{24,16},{1,9},{9,1},{17,25},{25,17},{2,10},{10... | collective-permute-start | bytes 3932168 | tf_op jit(solution)/shard_map/ppermute | solution.py:107
  96.1 89.8 %all-to-all-start = ((f32[8,2,40,1280]{3,2,1,0:T(8,128)}), f32[8,2,40,1280]{3,2,1,0:T(8,128)}, u32[]{:S(2)}, u32[]{:S(2)}) async-start(f32[8,2,40,1280]{3,2,1,0:T(8,128)} %reshape.401), calls=%async_computation | async-start | bytes 6553600 | tf_op jit(solution)/shard_map/all_to_all | solution.py:115
  106.6 31.1 %collective-permute-start.5 = (f32[2,8,160,128]{3,2,1,0:T(8,128)S(1)}, f32[2,8,160,128]{3,2,1,0:T(8,128)S(1)}, u32[]{:S(2)}, u32[]{:S(2)}) collective-permute-start(f32[2,8,160,128]{3,2,1,0:T(8,128)S(1)} %fusion.157), channel_id=1, source_target_pairs={{0,24},{8,16},{16,8},{24,0},{1,25},{9,17},{17,9},{25,1},{2,26},{10... | collective-permute-start | bytes 3932168 | tf_op jit(solution)/shard_map/ppermute | solution.py:107
  120.6 45.2 %collective-permute-start.4 = (f32[2,8,160,128]{3,2,1,0:T(8,128)S(1)}, f32[2,8,160,128]{3,2,1,0:T(8,128)S(1)}, u32[]{:S(2)}, u32[]{:S(2)}) collective-permute-start(f32[2,8,160,128]{3,2,1,0:T(8,128)S(1)} %fusion.154), channel_id=1, source_target_pairs={{0,16},{8,24},{16,0},{24,8},{1,17},{9,25},{17,1},{25,9},{2,18},{10... | collective-permute-start | bytes 3932168 | tf_op jit(solution)/shard_map/ppermute | solution.py:107
  123.6 42.2 %copy-start.15 = (f32[1,1,8,40,4,128]{5,3,1,4,2,0:T(8,128)S(1)}, f32[1,1,8,40,4,128]{5,3,1,4,2,0:T(8,128)}, u32[]{:S(2)}) copy-start(f32[1,1,8,40,4,128]{5,3,1,4,2,0:T(8,128)} %copy-done.14) | copy-start | bytes 1966084
  123.6 42.2 %copy-start.23 = (f32[1,1,8,40,4,128]{5,3,1,4,2,0:T(8,128)S(1)}, f32[1,1,8,40,4,128]{5,3,1,4,2,0:T(8,128)}, u32[]{:S(2)}) copy-start(f32[1,1,8,40,4,128]{5,3,1,4,2,0:T(8,128)} %copy-done.22) | copy-start | bytes 1966084
  123.6 42.2 %collective-permute-start.3 = (f32[2,8,160,128]{3,2,1,0:T(8,128)S(1)}, f32[2,8,160,128]{3,2,1,0:T(8,128)S(1)}, u32[]{:S(2)}, u32[]{:S(2)}) collective-permute-start(f32[2,8,160,128]{3,2,1,0:T(8,128)S(1)} %fusion.151), channel_id=1, source_target_pairs={{0,8},{8,0},{16,24},{24,16},{1,9},{9,1},{17,25},{25,17},{2,10},{10... | collective-permute-start | bytes 3932168 | tf_op jit(solution)/shard_map/ppermute | solution.py:107
  185.8 97.7 %all-to-all-start.1 = ((f32[8,2,40,1280]{3,2,1,0:T(8,128)}), f32[8,2,40,1280]{3,2,1,0:T(8,128)}, u32[]{:S(2)}, u32[]{:S(2)}) async-start(f32[8,2,40,1280]{3,2,1,0:T(8,128)} %reshape.405), calls=%async_computation.1 | async-start | bytes 6553600 | tf_op jit(solution)/shard_map/all_to_all | solution.py:115
  204.4 31.1 %collective-permute-start.8 = (f32[2,8,160,128]{3,2,1,0:T(8,128)S(1)}, f32[2,8,160,128]{3,2,1,0:T(8,128)S(1)}, u32[]{:S(2)}, u32[]{:S(2)}) collective-permute-start(f32[2,8,160,128]{3,2,1,0:T(8,128)S(1)} %fusion.169), channel_id=1, source_target_pairs={{0,24},{8,16},{16,8},{24,0},{1,25},{9,17},{17,9},{25,1},{2,26},{10... | collective-permute-start | bytes 3932168 | tf_op jit(solution)/shard_map/ppermute | solution.py:107
  207.5 56.1 %collective-permute-start.7 = (f32[2,8,160,128]{3,2,1,0:T(8,128)S(1)}, f32[2,8,160,128]{3,2,1,0:T(8,128)S(1)}, u32[]{:S(2)}, u32[]{:S(2)}) collective-permute-start(f32[2,8,160,128]{3,2,1,0:T(8,128)S(1)} %fusion.166), channel_id=1, source_target_pairs={{0,16},{8,24},{16,0},{24,8},{1,17},{9,25},{17,1},{25,9},{2,18},{10... | collective-permute-start | bytes 3932168 | tf_op jit(solution)/shard_map/ppermute | solution.py:107
  210.7 52.9 %copy-start.16 = (f32[1,1,8,40,4,128]{5,3,1,4,2,0:T(8,128)S(1)}, f32[1,1,8,40,4,128]{5,3,1,4,2,0:T(8,128)}, u32[]{:S(2)}) copy-start(f32[1,1,8,40,4,128]{5,3,1,4,2,0:T(8,128)} %copy-done.14) | copy-start | bytes 1966084
  210.7 52.9 %copy-start.24 = (f32[1,1,8,40,4,128]{5,3,1,4,2,0:T(8,128)S(1)}, f32[1,1,8,40,4,128]{5,3,1,4,2,0:T(8,128)}, u32[]{:S(2)}) copy-start(f32[1,1,8,40,4,128]{5,3,1,4,2,0:T(8,128)} %copy-done.22) | copy-start | bytes 1966084
  210.8 52.8 %collective-permute-start.6 = (f32[2,8,160,128]{3,2,1,0:T(8,128)S(1)}, f32[2,8,160,128]{3,2,1,0:T(8,128)S(1)}, u32[]{:S(2)}, u32[]{:S(2)}) collective-permute-start(f32[2,8,160,128]{3,2,1,0:T(8,128)S(1)} %fusion.163), channel_id=1, source_target_pairs={{0,8},{8,0},{16,24},{24,16},{1,9},{9,1},{17,25},{25,17},{2,10},{10... | collective-permute-start | bytes 3932168 | tf_op jit(solution)/shard_map/ppermute | solution.py:107
  283.6 87.3 %all-to-all-start.2 = ((f32[8,2,40,1280]{3,2,1,0:T(8,128)}), f32[8,2,40,1280]{3,2,1,0:T(8,128)}, u32[]{:S(2)}, u32[]{:S(2)}) async-start(f32[8,2,40,1280]{3,2,1,0:T(8,128)} %reshape.409), calls=%async_computation.2 | async-start | bytes 6553600 | tf_op jit(solution)/shard_map/all_to_all | solution.py:115
  291.5 30.9 %collective-permute-start.11 = (f32[2,8,160,128]{3,2,1,0:T(8,128)S(1)}, f32[2,8,160,128]{3,2,1,0:T(8,128)S(1)}, u32[]{:S(2)}, u32[]{:S(2)}) collective-permute-start(f32[2,8,160,128]{3,2,1,0:T(8,128)S(1)} %fusion.181), channel_id=1, source_target_pairs={{0,24},{8,16},{16,8},{24,0},{1,25},{9,17},{17,9},{25,1},{2,26},{10... | collective-permute-start | bytes 3932168 | tf_op jit(solution)/shard_map/ppermute | solution.py:107
  303.8 46.8 %collective-permute-start.10 = (f32[2,8,160,128]{3,2,1,0:T(8,128)S(1)}, f32[2,8,160,128]{3,2,1,0:T(8,128)S(1)}, u32[]{:S(2)}, u32[]{:S(2)}) collective-permute-start(f32[2,8,160,128]{3,2,1,0:T(8,128)S(1)} %fusion.178), channel_id=1, source_target_pairs={{0,16},{8,24},{16,0},{24,8},{1,17},{9,25},{17,1},{25,9},{2,18},{10... | collective-permute-start | bytes 3932168 | tf_op jit(solution)/shard_map/ppermute | solution.py:107
  307.2 43.5 %copy-start.17 = (f32[1,1,8,40,4,128]{5,3,1,4,2,0:T(8,128)S(1)}, f32[1,1,8,40,4,128]{5,3,1,4,2,0:T(8,128)}, u32[]{:S(2)}) copy-start(f32[1,1,8,40,4,128]{5,3,1,4,2,0:T(8,128)} %copy-done.14) | copy-start | bytes 1966084
  307.3 43.4 %copy-start.25 = (f32[1,1,8,40,4,128]{5,3,1,4,2,0:T(8,128)S(1)}, f32[1,1,8,40,4,128]{5,3,1,4,2,0:T(8,128)}, u32[]{:S(2)}) copy-start(f32[1,1,8,40,4,128]{5,3,1,4,2,0:T(8,128)} %copy-done.22) | copy-start | bytes 1966084
  307.3 43.4 %collective-permute-start.9 = (f32[2,8,160,128]{3,2,1,0:T(8,128)S(1)}, f32[2,8,160,128]{3,2,1,0:T(8,128)S(1)}, u32[]{:S(2)}, u32[]{:S(2)}) collective-permute-start(f32[2,8,160,128]{3,2,1,0:T(8,128)S(1)} %fusion.175), channel_id=1, source_target_pairs={{0,8},{8,0},{16,24},{24,16},{1,9},{9,1},{17,25},{25,17},{2,10},{10... | collective-permute-start | bytes 3932168 | tf_op jit(solution)/shard_map/ppermute | solution.py:107
  370.8 95.4 %all-to-all-start.3 = ((f32[8,2,40,1280]{3,2,1,0:T(8,128)}), f32[8,2,40,1280]{3,2,1,0:T(8,128)}, u32[]{:S(2)}, u32[]{:S(2)}) async-start(f32[8,2,40,1280]{3,2,1,0:T(8,128)} %reshape.413), calls=%async_computation.3 | async-start | bytes 6553600 | tf_op jit(solution)/shard_map/all_to_all | solution.py:115
  387.0 31.0 %collective-permute-start.14 = (f32[2,8,160,128]{3,2,1,0:T(8,128)S(1)}, f32[2,8,160,128]{3,2,1,0:T(8,128)S(1)}, u32[]{:S(2)}, u32[]{:S(2)}) collective-permute-start(f32[2,8,160,128]{3,2,1,0:T(8,128)S(1)} %fusion.193), channel_id=1, source_target_pairs={{0,24},{8,16},{16,8},{24,0},{1,25},{9,17},{17,9},{25,1},{2,26},{10... | collective-permute-start | bytes 3932168 | tf_op jit(solution)/shard_map/ppermute | solution.py:107
  390.1 56.2 %collective-permute-start.13 = (f32[2,8,160,128]{3,2,1,0:T(8,128)S(1)}, f32[2,8,160,128]{3,2,1,0:T(8,128)S(1)}, u32[]{:S(2)}, u32[]{:S(2)}) collective-permute-start(f32[2,8,160,128]{3,2,1,0:T(8,128)S(1)} %fusion.190), channel_id=1, source_target_pairs={{0,16},{8,24},{16,0},{24,8},{1,17},{9,25},{17,1},{25,9},{2,18},{10... | collective-permute-start | bytes 3932168 | tf_op jit(solution)/shard_map/ppermute | solution.py:107
  393.5 52.8 %collective-permute-start.12 = (f32[2,8,160,128]{3,2,1,0:T(8,128)S(1)}, f32[2,8,160,128]{3,2,1,0:T(8,128)S(1)}, u32[]{:S(2)}, u32[]{:S(2)}) collective-permute-start(f32[2,8,160,128]{3,2,1,0:T(8,128)S(1)} %fusion.187), channel_id=1, source_target_pairs={{0,8},{8,0},{16,24},{24,16},{1,9},{9,1},{17,25},{25,17},{2,10},{10... | collective-permute-start | bytes 3932168 | tf_op jit(solution)/shard_map/ppermute | solution.py:107
  404.7 41.6 %copy-start.18 = (f32[1,1,8,40,4,128]{5,3,1,4,2,0:T(8,128)S(1)}, f32[1,1,8,40,4,128]{5,3,1,4,2,0:T(8,128)}, u32[]{:S(2)}) copy-start(f32[1,1,8,40,4,128]{5,3,1,4,2,0:T(8,128)} %copy-done.14) | copy-start | bytes 1966084
  404.7 41.6 %copy-start.26 = (f32[1,1,8,40,4,128]{5,3,1,4,2,0:T(8,128)S(1)}, f32[1,1,8,40,4,128]{5,3,1,4,2,0:T(8,128)}, u32[]{:S(2)}) copy-start(f32[1,1,8,40,4,128]{5,3,1,4,2,0:T(8,128)} %copy-done.22) | copy-start | bytes 1966084
  466.2 89.0 %all-to-all-start.4 = ((f32[8,2,40,1280]{3,2,1,0:T(8,128)}), f32[8,2,40,1280]{3,2,1,0:T(8,128)}, u32[]{:S(2)}, u32[]{:S(2)}) async-start(f32[8,2,40,1280]{3,2,1,0:T(8,128)} %reshape.417), calls=%async_computation.4 | async-start | bytes 6553600 | tf_op jit(solution)/shard_map/all_to_all | solution.py:115
  475.8 30.9 %collective-permute-start.17 = (f32[2,8,160,128]{3,2,1,0:T(8,128)S(1)}, f32[2,8,160,128]{3,2,1,0:T(8,128)S(1)}, u32[]{:S(2)}, u32[]{:S(2)}) collective-permute-start(f32[2,8,160,128]{3,2,1,0:T(8,128)S(1)} %fusion.205), channel_id=1, source_target_pairs={{0,24},{8,16},{16,8},{24,0},{1,25},{9,17},{17,9},{25,1},{2,26},{10... | collective-permute-start | bytes 3932168 | tf_op jit(solution)/shard_map/ppermute | solution.py:107
  486.3 48.7 %collective-permute-start.16 = (f32[2,8,160,128]{3,2,1,0:T(8,128)S(1)}, f32[2,8,160,128]{3,2,1,0:T(8,128)S(1)}, u32[]{:S(2)}, u32[]{:S(2)}) collective-permute-start(f32[2,8,160,128]{3,2,1,0:T(8,128)S(1)} %fusion.202), channel_id=1, source_target_pairs={{0,16},{8,24},{16,0},{24,8},{1,17},{9,25},{17,1},{25,9},{2,18},{10... | collective-permute-start | bytes 3932168 | tf_op jit(solution)/shard_map/ppermute | solution.py:107
  490.0 45.0 %copy-start.19 = (f32[1,1,8,40,4,128]{5,3,1,4,2,0:T(8,128)S(1)}, f32[1,1,8,40,4,128]{5,3,1,4,2,0:T(8,128)}, u32[]{:S(2)}) copy-start(f32[1,1,8,40,4,128]{5,3,1,4,2,0:T(8,128)} %copy-done.14) | copy-start | bytes 1966084
  490.0 45.0 %copy-start.27 = (f32[1,1,8,40,4,128]{5,3,1,4,2,0:T(8,128)S(1)}, f32[1,1,8,40,4,128]{5,3,1,4,2,0:T(8,128)}, u32[]{:S(2)}) copy-start(f32[1,1,8,40,4,128]{5,3,1,4,2,0:T(8,128)} %copy-done.22) | copy-start | bytes 1966084
  490.0 45.0 %collective-permute-start.15 = (f32[2,8,160,128]{3,2,1,0:T(8,128)S(1)}, f32[2,8,160,128]{3,2,1,0:T(8,128)S(1)}, u32[]{:S(2)}, u32[]{:S(2)}) collective-permute-start(f32[2,8,160,128]{3,2,1,0:T(8,128)S(1)} %fusion.199), channel_id=1, source_target_pairs={{0,8},{8,0},{16,24},{24,16},{1,9},{9,1},{17,25},{25,17},{2,10},{10... | collective-permute-start | bytes 3932168 | tf_op jit(solution)/shard_map/ppermute | solution.py:107
  555.1 89.3 %all-to-all-start.5 = ((f32[8,2,40,1280]{3,2,1,0:T(8,128)}), f32[8,2,40,1280]{3,2,1,0:T(8,128)}, u32[]{:S(2)}, u32[]{:S(2)}) async-start(f32[8,2,40,1280]{3,2,1,0:T(8,128)} %reshape.421), calls=%async_computation.5 | async-start | bytes 6553600 | tf_op jit(solution)/shard_map/all_to_all | solution.py:115
  565.3 31.0 %collective-permute-start.20 = (f32[2,8,160,128]{3,2,1,0:T(8,128)S(1)}, f32[2,8,160,128]{3,2,1,0:T(8,128)S(1)}, u32[]{:S(2)}, u32[]{:S(2)}) collective-permute-start(f32[2,8,160,128]{3,2,1,0:T(8,128)S(1)} %fusion.217), channel_id=1, source_target_pairs={{0,24},{8,16},{16,8},{24,0},{1,25},{9,17},{17,9},{25,1},{2,26},{10... | collective-permute-start | bytes 3932168 | tf_op jit(solution)/shard_map/ppermute | solution.py:107
  568.0 56.5 %collective-permute-start.19 = (f32[2,8,160,128]{3,2,1,0:T(8,128)S(1)}, f32[2,8,160,128]{3,2,1,0:T(8,128)S(1)}, u32[]{:S(2)}, u32[]{:S(2)}) collective-permute-start(f32[2,8,160,128]{3,2,1,0:T(8,128)S(1)} %fusion.214), channel_id=1, source_target_pairs={{0,16},{8,24},{16,0},{24,8},{1,17},{9,25},{17,1},{25,9},{2,18},{10... | collective-permute-start | bytes 3932168 | tf_op jit(solution)/shard_map/ppermute | solution.py:107
  571.7 52.8 %copy-start.20 = (f32[1,1,8,40,4,128]{5,3,1,4,2,0:T(8,128)S(1)}, f32[1,1,8,40,4,128]{5,3,1,4,2,0:T(8,128)}, u32[]{:S(2)}) copy-start(f32[1,1,8,40,4,128]{5,3,1,4,2,0:T(8,128)} %copy-done.14) | copy-start | bytes 1966084
  571.7 52.8 %copy-start.28 = (f32[1,1,8,40,4,128]{5,3,1,4,2,0:T(8,128)S(1)}, f32[1,1,8,40,4,128]{5,3,1,4,2,0:T(8,128)}, u32[]{:S(2)}) copy-start(f32[1,1,8,40,4,128]{5,3,1,4,2,0:T(8,128)} %copy-done.22) | copy-start | bytes 1966084
  571.7 52.8 %collective-permute-start.18 = (f32[2,8,160,128]{3,2,1,0:T(8,128)S(1)}, f32[2,8,160,128]{3,2,1,0:T(8,128)S(1)}, u32[]{:S(2)}, u32[]{:S(2)}) collective-permute-start(f32[2,8,160,128]{3,2,1,0:T(8,128)S(1)} %fusion.211), channel_id=1, source_target_pairs={{0,8},{8,0},{16,24},{24,16},{1,9},{9,1},{17,25},{25,17},{2,10},{10... | collective-permute-start | bytes 3932168 | tf_op jit(solution)/shard_map/ppermute | solution.py:107
  644.5 87.7 %all-to-all-start.6 = ((f32[8,2,40,1280]{3,2,1,0:T(8,128)}), f32[8,2,40,1280]{3,2,1,0:T(8,128)}, u32[]{:S(2)}, u32[]{:S(2)}) async-start(f32[8,2,40,1280]{3,2,1,0:T(8,128)} %reshape.425), calls=%async_computation.6 | async-start | bytes 6553600 | tf_op jit(solution)/shard_map/all_to_all | solution.py:115
  653.1 30.9 %collective-permute-start.23 = (f32[2,8,160,128]{3,2,1,0:T(8,128)S(1)}, f32[2,8,160,128]{3,2,1,0:T(8,128)S(1)}, u32[]{:S(2)}, u32[]{:S(2)}) collective-permute-start(f32[2,8,160,128]{3,2,1,0:T(8,128)S(1)} %fusion.229), channel_id=1, source_target_pairs={{0,24},{8,16},{16,8},{24,0},{1,25},{9,17},{17,9},{25,1},{2,26},{10... | collective-permute-start | bytes 3932168 | tf_op jit(solution)/shard_map/ppermute | solution.py:107
  655.6 56.7 %collective-permute-start.22 = (f32[2,8,160,128]{3,2,1,0:T(8,128)S(1)}, f32[2,8,160,128]{3,2,1,0:T(8,128)S(1)}, u32[]{:S(2)}, u32[]{:S(2)}) collective-permute-start(f32[2,8,160,128]{3,2,1,0:T(8,128)S(1)} %fusion.226), channel_id=1, source_target_pairs={{0,16},{8,24},{16,0},{24,8},{1,17},{9,25},{17,1},{25,9},{2,18},{10... | collective-permute-start | bytes 3932168 | tf_op jit(solution)/shard_map/ppermute | solution.py:107
  659.6 52.7 %copy-start.21 = (f32[1,1,8,40,4,128]{5,3,1,4,2,0:T(8,128)S(1)}, f32[1,1,8,40,4,128]{5,3,1,4,2,0:T(8,128)}, u32[]{:S(2)}) copy-start(f32[1,1,8,40,4,128]{5,3,1,4,2,0:T(8,128)} %copy-done.14) | copy-start | bytes 1966084
  659.6 52.7 %copy-start.29 = (f32[1,1,8,40,4,128]{5,3,1,4,2,0:T(8,128)S(1)}, f32[1,1,8,40,4,128]{5,3,1,4,2,0:T(8,128)}, u32[]{:S(2)}) copy-start(f32[1,1,8,40,4,128]{5,3,1,4,2,0:T(8,128)} %copy-done.22) | copy-start | bytes 1966084
  659.6 52.7 %collective-permute-start.21 = (f32[2,8,160,128]{3,2,1,0:T(8,128)S(1)}, f32[2,8,160,128]{3,2,1,0:T(8,128)S(1)}, u32[]{:S(2)}, u32[]{:S(2)}) collective-permute-start(f32[2,8,160,128]{3,2,1,0:T(8,128)S(1)} %fusion.223), channel_id=1, source_target_pairs={{0,8},{8,0},{16,24},{24,16},{1,9},{9,1},{17,25},{25,17},{2,10},{10... | collective-permute-start | bytes 3932168 | tf_op jit(solution)/shard_map/ppermute | solution.py:107
  732.2 97.4 %all-to-all-start.7 = ((f32[8,2,40,1280]{3,2,1,0:T(8,128)}), f32[8,2,40,1280]{3,2,1,0:T(8,128)}, u32[]{:S(2)}, u32[]{:S(2)}) async-start(f32[8,2,40,1280]{3,2,1,0:T(8,128)} %reshape.429), calls=%async_computation.7 | async-start | bytes 6553600 | tf_op jit(solution)/shard_map/all_to_all | solution.py:115
  853.0 40.4 %slice-start.8 = ((s8[5242880]{0:T(1024)(128)(4,1)}), s8[4194304]{0:T(1024)(128)(4,1)S(1)}, s32[]{:S(2)}) async-start(s8[5242880]{0:T(1024)(128)(4,1)} %bitcast.502), calls=%async_computation.16 | async-start | bytes 8388608
  873.2 40.4 %slice-start.6 = ((s8[5242880]{0:T(1024)(128)(4,1)}), s8[4194304]{0:T(1024)(128)(4,1)S(1)}, s32[]{:S(2)}) async-start(s8[5242880]{0:T(1024)(128)(4,1)} %bitcast.499), calls=%async_computation.14 | async-start | bytes 8388608
  (28 other events, 426.4 us)
